TPU v7x, 32 devices: a whole 2x2x4 slice. The times are simulated.
32 devices in a mesh: pa: 8 (over z, x), sa: 4 (over y, core).
Axes of the slice: x: 2, y: 2, z: 4, core: 2. Of those that a mesh axis runs over, the one named last changes fastest.
Arguments:
- factors: bfloat16 [64, 16, 1024], P(None, None, 'pa'), may hold values from -6 to 6
- trade_weights: bfloat16 [64, 8192], P(None, 'pa'), may hold values from -0.75 to 0.75
- payoff_terms: bfloat16 [2, 8192], P(None, 'pa'), may hold values from -6 to 6
- set_blocks: int32 [32], replicated, may hold values from 1 to 4, 64 in all
- shock_pick: int32 [8], P('sa'), may hold values from 0 to 31
- shock_scale: float32 [32, 64], replicated, may hold values from 0.25 to 1.75
- shock_shift: float32 [32, 64], replicated, may hold values from -3 to 3
- discount: bfloat16 [16, 1024], P(None, 'pa'), may hold values from 0.5 to 1
- set_pd: float32 [32, 16], P('pa'), may hold values from 0.02 to 0.2
- own_pd: float32 [16], replicated, may hold values from 0.02 to 0.2
Outputs:
- exposure_profile: float32 [2, 32, 16, 8], P(None, 'pa', None, 'sa')
- set_xva: float32 [32, 8], P('pa', 'sa')
- total_xva: float32 [8], P('sa')
Inputs may be any that keep to these rules, and one draw needn't show every extreme that they name: `set_blocks`: each of the 32 netting sets holds whole consecutive blocks of 128 trades; the counts sum to 64.
All inputs are finite; a program needn't handle non-finite values.
Results may differ from a plain program's by a relative error of at most 0.00046.
Values may be sent and summed in bfloat16 or wider, within the bound.
A program may use at most 64 MiB of HBM per device.

v0:
```python
import functools
import math

import jax
import jax.numpy as jnp
from jax import lax
from jax.experimental import pallas as pl
from jax.experimental.pallas import tpu as pltpu
from jax.sharding import PartitionSpec as P

UNIT_SCALE = 0.0625
LOG2E = 1.0 / math.log(2.0)
BLOCK = 128
BF = jnp.bfloat16
F32 = jnp.float32
CEIL = 100.0
KDIM = 128
SUB = 256


def pick_column(library_ref, row):
    count, width = library_ref.shape
    rows = lax.broadcasted_iota(jnp.int32, (count, width), 0)
    line = jnp.sum(jnp.where(rows == row, library_ref[...], 0.0), axis=0, keepdims=True)
    square = jnp.broadcast_to(line, (width, width))
    eye = lax.broadcasted_iota(jnp.int32, (width, width), 0) == lax.broadcasted_iota(
        jnp.int32, (width, width), 1
    )
    return jnp.sum(jnp.where(eye, square, 0.0), axis=1, keepdims=True)


def shock_rows(factor_ref, pick_ref, scale_ref, shift_ref, wide_ref, shocked_ref):
    factors, dates, paths = factor_ref.shape
    shocks = pick_ref.shape[0]
    for k in range(factors):
        wide_ref[k * dates : (k + 1) * dates, :] = factor_ref[k].astype(F32)
    rest = shocked_ref.shape[0] - factors
    ones = lax.broadcasted_iota(jnp.int32, (rest, shocked_ref.shape[1]), 0) < 2
    shocked_ref[factors:, :] = jnp.where(ones, 1.0, 0.0).astype(BF)
    for s in range(shocks):
        scale = pick_column(scale_ref, pick_ref[s]) * LOG2E
        shift = pick_column(shift_ref, pick_ref[s]) * LOG2E
        scale = jnp.broadcast_to(scale, (factors, paths))
        shift = jnp.broadcast_to(shift, (factors, paths))
        for d in range(dates):
            line = wide_ref[pl.ds(d, factors, stride=dates), :]
            at = (d * shocks + s) * paths
            shocked_ref[:factors, at : at + paths] = (scale * line + shift).astype(BF)


def load_trades(weights, terms, factors):
    strike = terms[1:2].astype(F32) * LOG2E
    high = strike.astype(BF).astype(F32)
    low = strike - high
    width = weights.shape[1]
    rest = jnp.zeros((KDIM - factors - 8, width), F32)
    row = lax.broadcasted_iota(jnp.int32, (8, width), 0)
    tail = jnp.where(row == 0, high, jnp.where(row == 1, low, 0.0))
    stack = jnp.concatenate([weights.astype(F32), tail, rest], axis=0)
    return stack.T.astype(BF)


def send(source, target, send_sem, recv_sem, place):
    return pltpu.make_async_remote_copy(
        src_ref=source,
        dst_ref=target,
        send_sem=send_sem,
        recv_sem=recv_sem,
        device_id=place,
        device_id_type=pl.DeviceIdType.MESH,
    )


def kernel(
    groups,
    lanes_across,
    pick_ref,
    factor_ref,
    weight_ref,
    term_ref,
    block_ref,
    scale_ref,
    shift_ref,
    discount_ref,
    pd_ref,
    own_ref,
    out_ref,
    wide_ref,
    shocked_ref,
    loading_ref,
    member_ref,
    net_ref,
    weight_all,
    term_all,
    pd_all,
    message_ref,
    inbox_ref,
    send_sem,
    recv_sem,
    post_sem,
    inbox_sem,
):
    factors, dates, paths = factor_ref.shape
    shocks = pick_ref.shape[0]
    local = weight_ref.shape[1]
    sets = block_ref.shape[1]
    owned = pd_ref.shape[0]
    across = lanes_across
    devices = groups * across
    me_p = lax.axis_index("pa")
    me_s = lax.axis_index("sa")
    me = me_p * across + me_s
    parts = ((weight_ref, weight_all), (term_ref, term_all), (pd_ref, pd_all))

    barrier = pltpu.get_barrier_semaphore()

    def greet(step, _):
        other = lax.rem(me + step, devices)
        pl.semaphore_signal(
            barrier,
            inc=1,
            device_id=(other // across, lax.rem(other, across)),
            device_id_type=pl.DeviceIdType.MESH,
        )
        return 0

    lax.fori_loop(1, devices, greet, 0)
    for n, (source, target) in enumerate(parts):
        pltpu.make_async_copy(source, target.at[me_p], recv_sem.at[n, me_p]).start()
    shock_rows(factor_ref, pick_ref, scale_ref, shift_ref, wide_ref, shocked_ref)
    pl.semaphore_wait(barrier, devices - 1)

    def gather(step):
        other = lax.rem(me_p - step + groups, groups)
        return [
            send(source, target.at[me_p], send_sem.at[n, step], recv_sem.at[n, me_p], (other, me_s))
            for n, (source, target) in enumerate(parts)
        ]

    for step in range(1, groups):
        for copy in gather(step):
            copy.start()

    m = lax.broadcasted_iota(jnp.int32, (sets, sets), 0)
    j = lax.broadcasted_iota(jnp.int32, (sets, sets), 1)
    counts = jnp.broadcast_to(block_ref[...].astype(F32), (sets, sets))
    ends = jnp.sum(jnp.where(j <= m, counts, 0.0), axis=1, keepdims=True) * BLOCK
    begins = jnp.sum(jnp.where(j < m, counts, 0.0), axis=1, keepdims=True) * BLOCK
    net_ref[...] = jnp.zeros_like(net_ref)
    wide = shocks * paths
    unroll = 8 if dates % 8 == 0 else 1
    sub = min(SUB, local)

    def one_slot(step, _):
        slot = lax.rem(me_p + step, groups)
        for n, (source, target) in enumerate(parts):
            pltpu.make_async_copy(source, target.at[slot], recv_sem.at[n, slot]).wait()
        terms = term_all[slot]
        loading_ref[...] = load_trades(weight_all[slot], terms, factors)
        ids = lax.broadcasted_iota(jnp.int32, (sets, local), 1) + slot * local
        ids = ids.astype(F32)
        notional = jnp.broadcast_to(terms[0:1].astype(F32), (sets, local))
        inside = jnp.logical_and(ids >= begins, ids < ends)
        member_ref[...] = jnp.where(inside, notional, 0.0).astype(BF)

        def some_dates(turn, _):
            for d in range(unroll):
                at = pl.multiple_of((turn * unroll + d) * wide, wide)
                columns = shocked_ref[:, pl.ds(at, wide)]
                values = []
                for r in range(0, local, sub):
                    part = loading_ref[r : r + sub, :]
                    u = jnp.dot(part, columns, preferred_element_type=F32).astype(BF)
                    grown = jnp.exp2(jnp.minimum(u, jnp.asarray(CEIL, BF)))
                    values.append(jnp.maximum(jnp.log2(grown + jnp.asarray(1.0, BF)), u))
                whole = jnp.concatenate(values, axis=0)
                net_ref[:, pl.ds(at, wide)] += jnp.dot(
                    member_ref[...], whole, preferred_element_type=F32
                )
            return 0

        lax.fori_loop(0, dates // unroll, some_dates, 0)
        return 0

    lax.fori_loop(0, groups, one_slot, 0)

    count = dates * shocks
    lane = lax.broadcasted_iota(jnp.int32, (sets, 128), 1)
    sums = jnp.zeros((sets, 128), F32)
    total_paths = paths * groups
    for d in range(dates):
        cheap = discount_ref[d : d + 1, :].astype(F32) * (UNIT_SCALE * math.log(2.0))
        for s in range(shocks):
            at = d * wide + s * paths
            exposure = net_ref[:, at : at + paths] * cheap
            up = jnp.sum(jnp.maximum(exposure, 0.0), axis=1, keepdims=True)
            down = jnp.sum(jnp.minimum(exposure, 0.0), axis=1, keepdims=True)
            sums = jnp.where(lane == s * dates + d, up, sums)
            sums = jnp.where(lane == count + s * dates + d, down, sums)
    sums = sums / total_paths

    rest = jnp.zeros((owned, 128 - 2 * count), F32)
    own = [jnp.broadcast_to(own_ref[...], (owned, dates))] * shocks
    small = lax.broadcasted_iota(jnp.int32, (owned, 128), 1)

    def of_shock(s):
        up = jnp.logical_and(small >= s * dates, small < (s + 1) * dates)
        down = jnp.logical_and(small >= count + s * dates, small < count + (s + 1) * dates)
        return jnp.logical_or(up, down)

    totals = [jnp.zeros((1, 1), F32)] * shocks
    blocks = []
    for q in range(groups):
        rows = sums[q * owned : (q + 1) * owned, :]
        prices = jnp.concatenate([pd_all[q]] * shocks + own + [rest], axis=1)
        part = prices * rows
        both = jnp.sum(part, axis=1, keepdims=True)
        blocks.append(jnp.where(small == 2 * count, both, rows))
        for s in range(shocks):
            picked = jnp.sum(jnp.where(of_shock(s), part, 0.0), axis=1, keepdims=True)
            totals[s] = totals[s] + jnp.sum(picked, axis=0, keepdims=True)
    for q in range(groups):
        block = blocks[q]
        for s in range(shocks):
            block = jnp.where(small == 2 * count + 1 + s, totals[s], block)
        message_ref[q] = block
    inbox_ref[me_p, me_s] = message_ref[me_p]

    def post(step):
        other = lax.rem(me + step, devices)
        other_p = other // across
        return send(
            message_ref.at[other_p],
            inbox_ref.at[me_p, me_s],
            post_sem.at[step],
            inbox_sem.at[me],
            (other_p, lax.rem(other, across)),
        )

    def post_one(step, _):
        post(step).start()
        return 0

    def take_one(step, _):
        source = lax.rem(me + step, devices)
        pltpu.make_async_copy(
            message_ref.at[0],
            inbox_ref.at[source // across, lax.rem(source, across)],
            inbox_sem.at[source],
        ).wait()
        return 0

    def done_one(step, _):
        post(step).wait_send()
        return 0

    lax.fori_loop(1, devices, post_one, 0)
    for step in range(1, groups):
        for copy in gather(step):
            copy.wait_send()
    lax.fori_loop(1, devices, take_one, 0)

    mine = jnp.zeros((owned, 128), F32)
    every = jnp.zeros((owned, 128), F32)
    for q in range(groups):
        mine = mine + inbox_ref[q, me_s]
        for s in range(across):
            every = every + inbox_ref[q, s]
    mean = jnp.sum(jnp.where(small == 2 * count, every, 0.0), axis=1, keepdims=True)
    mean = mean / (shocks * across)
    part = jnp.concatenate([pd_ref[...]] * shocks + own + [rest], axis=1) * mine
    for s in range(shocks):
        adjustment = jnp.sum(jnp.where(of_shock(s), part, 0.0), axis=1, keepdims=True)
        mine = jnp.where(small == 2 * count + 1 + shocks + s, adjustment - mean, mine)
    out_ref[...] = mine
    lax.fori_loop(1, devices, done_one, 0)


def on_device(
    factors,
    trade_weights,
    payoff_terms,
    set_blocks,
    shock_pick,
    shock_scale,
    shock_shift,
    discount,
    set_pd,
    own_pd,
):
    sets = set_blocks.shape[0]
    owned = set_pd.shape[0]
    count, dates, paths = factors.shape
    shocks = shock_pick.shape[0]
    groups = lax.axis_size("pa")
    across = lax.axis_size("sa")
    local = trade_weights.shape[1]
    vmem = pl.BlockSpec(memory_space=pltpu.VMEM)
    smem = pl.BlockSpec(memory_space=pltpu.SMEM)
    result = pl.pallas_call(
        functools.partial(kernel, groups, across),
        out_shape=jax.ShapeDtypeStruct((owned, 128), F32),
        in_specs=[smem] + [vmem] * 9,
        out_specs=vmem,
        scratch_shapes=[
            pltpu.VMEM((count * dates, paths), F32),
            pltpu.VMEM((KDIM, dates * shocks * paths), BF),
            pltpu.VMEM((local, KDIM), BF),
            pltpu.VMEM((sets, local), BF),
            pltpu.VMEM((sets, dates * shocks * paths), F32),
            pltpu.VMEM((groups,) + trade_weights.shape, BF),
            pltpu.VMEM((groups,) + payoff_terms.shape, BF),
            pltpu.VMEM((groups,) + set_pd.shape, F32),
            pltpu.VMEM((groups, owned, 128), F32),
            pltpu.VMEM((groups, across, owned, 128), F32),
            pltpu.SemaphoreType.DMA((3, groups)),
            pltpu.SemaphoreType.DMA((3, groups)),
            pltpu.SemaphoreType.DMA((groups * across,)),
            pltpu.SemaphoreType.DMA((groups * across,)),
        ],
        compiler_params=pltpu.CompilerParams(
            vmem_limit_bytes=48 * 1024 * 1024, collective_id=0, has_side_effects=True
        ),
    )(
        shock_pick,
        factors,
        trade_weights,
        payoff_terms,
        set_blocks[None, :],
        shock_scale,
        shock_shift,
        discount,
        set_pd,
        own_pd[None, :],
    )
    lanes = dates * shocks
    profile = result[:, : 2 * lanes].reshape(owned, 2, shocks, dates)
    profile = profile.transpose(1, 0, 3, 2)
    total_xva = result[0, 2 * lanes + 1 : 2 * lanes + 1 + shocks]
    set_xva = result[:, 2 * lanes + 1 + shocks : 2 * lanes + 1 + 2 * shocks]
    return (profile, set_xva, total_xva)


def solution(mesh):
    return jax.shard_map(
        on_device,
        mesh=mesh,
        in_specs=(
            P(None, None, "pa"),
            P(None, "pa"),
            P(None, "pa"),
            P(),
            P("sa"),
            P(),
            P(),
            P(None, "pa"),
            P("pa", None),
            P(),
        ),
        out_specs=(P(None, "pa", None, "sa"), P("pa", "sa"), P("sa")),
        check_vma=False,
    )
```

profile of v0, /device:TPU:0, one launch (start us, length us, event | category | flops | bytes accessed | tf_op | source)
XLA Modules:
  0.0 77.1 jit_solution(15809449306210777722)
XLA Ops:
  0.6 0.0 copy-start.6
  0.6 0.0 copy-start.7
  0.7 0.0 copy-start.8
  0.7 0.0 copy-start.9
  0.7 0.6 copy-done.6
  1.3 0.0 copy-done.7
  1.3 0.0 copy-done.8
  1.3 0.0 copy-done.9
  1.3 0.0 copy-start
  1.3 0.9 %copy-done = bf16[64,16,128]{2,1,0:T(8,128)(2,1)S(1)} copy-done((bf16[64,16,128]{2,1,0:T(8,128)(2,1)S(1)}, bf16[64,16,128]{2,1,0:T(8,128)(2,1)}, u32[]{:S(2)}) %copy-start) | copy-done | bytes 262168
  2.3 0.0 copy-start.1
  2.3 0.9 %copy-done.1 = bf16[64,1024]{1,0:T(8,128)(2,1)S(1)} copy-done((bf16[64,1024]{1,0:T(8,128)(2,1)S(1)}, bf16[64,1024]{1,0:T(8,128)(2,1)}, u32[]{:S(2)}) %copy-start.1) | copy-done | bytes 131096
  3.2 0.0 copy-start.2
  3.2 0.7 copy-done.2
  3.9 0.0 copy-start.3
  3.9 0.7 copy-done.3
  4.6 0.0 copy-start.4
  4.6 0.7 copy-done.4
  5.3 0.0 copy-start.5
  5.3 0.7 copy-done.5
  6.0 69.1 %shard_map.121 = f32[4,128]{1,0:T(4,128)S(1)} custom-call(s32[2]{0:T(128)S(1)} %copy-done.7, bf16[64,16,128]{2,1,0:T(8,128)(2,1)S(1)} %copy-done, bf16[64,1024]{1,0:T(8,128)(2,1)S(1)} %copy-done.1, bf16[2,1024]{1,0:T(2,128)(2,1)S(1)} %copy-done.4, s32[1,32]{1,0:T(1,128)S(1)} %bitcast.9, f32[32,64]{1,0:T(8,128)S(1)} %copy-done.2, f32[32,64]{1,0:T(8,128)S(1)} %copy-done.3, ...), custom_call_target="tpu_custom_call" | custom-call | tf_op jit(solution)/shard_map/pallas_call | solution.py:300
  75.1 0.6 slice_bitcast_fusion
  75.7 0.1 slice.10
  75.8 0.7 copy.14
  76.4 0.1 reshape.9
  76.5 0.6 copy.16
Async XLA Ops:
  0.6 0.7 copy-start.6
  0.6 0.7 copy-start.7
  0.7 0.7 copy-start.8
  0.7 0.7 copy-start.9
  1.3 0.9 %copy-start = (bf16[64,16,128]{2,1,0:T(8,128)(2,1)S(1)}, bf16[64,16,128]{2,1,0:T(8,128)(2,1)}, u32[]{:S(2)}) copy-start(bf16[64,16,128]{2,1,0:T(8,128)(2,1)} %factor_ref.1) | copy-start | bytes 786436
  2.3 0.9 %copy-start.1 = (bf16[64,1024]{1,0:T(8,128)(2,1)S(1)}, bf16[64,1024]{1,0:T(8,128)(2,1)}, u32[]{:S(2)}) copy-start(bf16[64,1024]{1,0:T(8,128)(2,1)} %weight_ref.1) | copy-start | bytes 393220
  3.2 0.7 copy-start.2
  3.9 0.7 copy-start.3
  4.6 0.7 copy-start.4
  5.3 0.7 copy-start.5
where the time goes:
time: 77.5 us; the launch traced here: 77.1 us
  Pallas kernels  69.1 us (89%)
  local copies, waits for them, and re-layouts  7.32 us (9%)
    pallas_call x1, Pallas kernels, on_device(): pl.pallas_call(functools.partial(kernel, groups, across), out_shape=jax.S...  69.1 us
    unnamed x21, local copies, waits for them, and re-layouts  5.98 us

commit v1 on v0

--- a/solution.py
+++ b/solution.py
@@ -15,7 +15,7 @@
 F32 = jnp.float32
 CEIL = 100.0
 KDIM = 128
-SUB = 256
+SUB = 128
 
 
 def pick_column(library_ref, row):
@@ -170,9 +170,9 @@
                 values = []
                 for r in range(0, local, sub):
                     part = loading_ref[r : r + sub, :]
-                    u = jnp.dot(part, columns, preferred_element_type=F32).astype(BF)
-                    grown = jnp.exp2(jnp.minimum(u, jnp.asarray(CEIL, BF)))
-                    values.append(jnp.maximum(jnp.log2(grown + jnp.asarray(1.0, BF)), u))
+                    u = jnp.dot(part, columns, preferred_element_type=F32)
+                    grown = jnp.exp2(jnp.minimum(u, CEIL))
+                    values.append(jnp.maximum(jnp.log2(grown + 1.0), u).astype(BF))
                 whole = jnp.concatenate(values, axis=0)
                 net_ref[:, pl.ds(at, wide)] += jnp.dot(
                     member_ref[...], whole, preferred_element_type=F32

time: 77.5 us -> 71.8 us (0.926)
  Pallas kernels: 69.1 us -> 63.4 us
    pallas_call x1, Pallas kernels: 69.1 us -> 63.4 us  [on_device(): pl.pallas_call(functools.partial(kernel, groups, across), out_shape=jax.S...]
where the time goes in v1:
time: 71.8 us; the launch traced here: 71.4 us
  Pallas kernels  63.4 us (88%)
  local copies, waits for them, and re-layouts  7.32 us (10%)
    pallas_call x1, Pallas kernels, on_device(): pl.pallas_call(functools.partial(kernel, groups, across), out_shape=jax.S...  63.4 us
    unnamed x21, local copies, waits for them, and re-layouts  5.98 us

profile of v1, /device:TPU:0, one launch (start us, length us, event | category | flops | bytes accessed | tf_op | source)
XLA Modules:
  0.0 71.4 jit_solution(8948128871699127892)
XLA Ops:
  0.6 0.0 copy-start.6
  0.6 0.0 copy-start.7
  0.7 0.0 copy-start.8
  0.7 0.0 copy-start.9
  0.7 0.6 copy-done.6
  1.3 0.0 copy-done.7
  1.3 0.0 copy-done.8
  1.3 0.0 copy-done.9
  1.3 0.0 copy-start
  1.3 0.9 %copy-done = bf16[64,16,128]{2,1,0:T(8,128)(2,1)S(1)} copy-done((bf16[64,16,128]{2,1,0:T(8,128)(2,1)S(1)}, bf16[64,16,128]{2,1,0:T(8,128)(2,1)}, u32[]{:S(2)}) %copy-start) | copy-done | bytes 262168
  2.3 0.0 copy-start.1
  2.3 0.9 %copy-done.1 = bf16[64,1024]{1,0:T(8,128)(2,1)S(1)} copy-done((bf16[64,1024]{1,0:T(8,128)(2,1)S(1)}, bf16[64,1024]{1,0:T(8,128)(2,1)}, u32[]{:S(2)}) %copy-start.1) | copy-done | bytes 131096
  3.2 0.0 copy-start.2
  3.2 0.7 %copy-done.2 = f32[32,64]{1,0:T(8,128)S(1)} copy-done((f32[32,64]{1,0:T(8,128)S(1)}, f32[32,64]{1,0:T(8,128)}, u32[]{:S(2)}) %copy-start.2) | copy-done | bytes 8216
  3.9 0.0 copy-start.3
  3.9 0.7 %copy-done.3 = f32[32,64]{1,0:T(8,128)S(1)} copy-done((f32[32,64]{1,0:T(8,128)S(1)}, f32[32,64]{1,0:T(8,128)}, u32[]{:S(2)}) %copy-start.3) | copy-done | bytes 8216
  4.6 0.0 copy-start.4
  4.6 0.7 copy-done.4
  5.3 0.0 copy-start.5
  5.3 0.7 copy-done.5
  6.0 63.4 %shard_map.121 = f32[4,128]{1,0:T(4,128)S(1)} custom-call(s32[2]{0:T(128)S(1)} %copy-done.7, bf16[64,16,128]{2,1,0:T(8,128)(2,1)S(1)} %copy-done, bf16[64,1024]{1,0:T(8,128)(2,1)S(1)} %copy-done.1, bf16[2,1024]{1,0:T(2,128)(2,1)S(1)} %copy-done.4, s32[1,32]{1,0:T(1,128)S(1)} %bitcast.9, f32[32,64]{1,0:T(8,128)S(1)} %copy-done.2, f32[32,64]{1,0:T(8,128)S(1)} %copy-done.3, ...), custom_call_target="tpu_custom_call" | custom-call | tf_op jit(solution)/shard_map/pallas_call | solution.py:300
  69.4 0.6 slice_bitcast_fusion
  70.0 0.1 slice.10
  70.0 0.7 copy.14
  70.7 0.1 reshape.9
  70.8 0.6 copy.16
Async XLA Ops:
  0.6 0.7 copy-start.6
  0.6 0.7 copy-start.7
  0.7 0.7 copy-start.8
  0.7 0.7 copy-start.9
  1.3 0.9 %copy-start = (bf16[64,16,128]{2,1,0:T(8,128)(2,1)S(1)}, bf16[64,16,128]{2,1,0:T(8,128)(2,1)}, u32[]{:S(2)}) copy-start(bf16[64,16,128]{2,1,0:T(8,128)(2,1)} %factor_ref.1) | copy-start | bytes 786436
  2.3 0.9 %copy-start.1 = (bf16[64,1024]{1,0:T(8,128)(2,1)S(1)}, bf16[64,1024]{1,0:T(8,128)(2,1)}, u32[]{:S(2)}) copy-start(bf16[64,1024]{1,0:T(8,128)(2,1)} %weight_ref.1) | copy-start | bytes 393220
  3.2 0.7 %copy-start.2 = (f32[32,64]{1,0:T(8,128)S(1)}, f32[32,64]{1,0:T(8,128)}, u32[]{:S(2)}) copy-start(f32[32,64]{1,0:T(8,128)} %scale_ref.1) | copy-start | bytes 24580
  3.9 0.7 %copy-start.3 = (f32[32,64]{1,0:T(8,128)S(1)}, f32[32,64]{1,0:T(8,128)}, u32[]{:S(2)}) copy-start(f32[32,64]{1,0:T(8,128)} %shift_ref.1) | copy-start | bytes 24580
  4.6 0.7 copy-start.4
  5.3 0.7 copy-start.5

commit v2 on v1

--- a/solution.py
+++ b/solution.py
@@ -60,6 +60,16 @@
     return stack.T.astype(BF)
 
 
+def partner(me, step, groups):
+    if groups & (groups - 1):
+        return lax.rem(me + step, groups)
+    other, bit = 0, 1
+    while bit < groups:
+        other = other + lax.rem(me // bit + step // bit, 2) * bit
+        bit = bit * 2
+    return other
+
+
 def send(source, target, send_sem, recv_sem, place):
     return pltpu.make_async_remote_copy(
         src_ref=source,
@@ -74,17 +84,24 @@
 def kernel(
     groups,
     lanes_across,
+    pick_hbm,
+    factor_hbm,
+    weight_hbm,
+    term_hbm,
+    block_hbm,
+    scale_hbm,
+    shift_hbm,
+    discount_hbm,
+    pd_hbm,
+    own_hbm,
+    out_ref,
     pick_ref,
     factor_ref,
-    weight_ref,
-    term_ref,
     block_ref,
     scale_ref,
     shift_ref,
     discount_ref,
-    pd_ref,
     own_ref,
-    out_ref,
     wide_ref,
     shocked_ref,
     loading_ref,
@@ -99,18 +116,37 @@
     recv_sem,
     post_sem,
     inbox_sem,
+    load_sem,
 ):
     factors, dates, paths = factor_ref.shape
     shocks = pick_ref.shape[0]
-    local = weight_ref.shape[1]
+    local = weight_hbm.shape[1]
     sets = block_ref.shape[1]
-    owned = pd_ref.shape[0]
+    owned = pd_hbm.shape[0]
     across = lanes_across
     devices = groups * across
     me_p = lax.axis_index("pa")
     me_s = lax.axis_index("sa")
     me = me_p * across + me_s
-    parts = ((weight_ref, weight_all), (term_ref, term_all), (pd_ref, pd_all))
+    parts = ((weight_hbm, weight_all), (term_hbm, term_all), (pd_hbm, pd_all))
+    early = [
+        pltpu.make_async_copy(source, target, load_sem.at[n])
+        for n, (source, target) in enumerate(
+            (
+                (pick_hbm, pick_ref),
+                (scale_hbm, scale_ref),
+                (shift_hbm, shift_ref),
+                (factor_hbm, factor_ref),
+                (block_hbm, block_ref),
+                (discount_hbm, discount_ref),
+                (own_hbm, own_ref),
+            )
+        )
+    ]
+    for copy in early:
+        copy.start()
+    for n, (source, target) in enumerate(parts):
+        pltpu.make_async_copy(source, target.at[me_p], recv_sem.at[n, me_p]).start()
 
     barrier = pltpu.get_barrier_semaphore()
 
@@ -125,21 +161,22 @@
         return 0
 
     lax.fori_loop(1, devices, greet, 0)
-    for n, (source, target) in enumerate(parts):
-        pltpu.make_async_copy(source, target.at[me_p], recv_sem.at[n, me_p]).start()
+    for copy in early:
+        copy.wait()
     shock_rows(factor_ref, pick_ref, scale_ref, shift_ref, wide_ref, shocked_ref)
-    pl.semaphore_wait(barrier, devices - 1)
 
     def gather(step):
-        other = lax.rem(me_p - step + groups, groups)
+        other = partner(me_p, step if not groups & (groups - 1) else groups - step, groups)
         return [
-            send(source, target.at[me_p], send_sem.at[n, step], recv_sem.at[n, me_p], (other, me_s))
+            send(
+                target.at[me_p],
+                target.at[me_p],
+                send_sem.at[n, step],
+                recv_sem.at[n, me_p],
+                (other, me_s),
+            )
             for n, (source, target) in enumerate(parts)
         ]
-
-    for step in range(1, groups):
-        for copy in gather(step):
-            copy.start()
 
     m = lax.broadcasted_iota(jnp.int32, (sets, sets), 0)
     j = lax.broadcasted_iota(jnp.int32, (sets, sets), 1)
@@ -152,7 +189,7 @@
     sub = min(SUB, local)
 
     def one_slot(step, _):
-        slot = lax.rem(me_p + step, groups)
+        slot = partner(me_p, step, groups)
         for n, (source, target) in enumerate(parts):
             pltpu.make_async_copy(source, target.at[slot], recv_sem.at[n, slot]).wait()
         terms = term_all[slot]
@@ -177,6 +214,14 @@
                 net_ref[:, pl.ds(at, wide)] += jnp.dot(
                     member_ref[...], whole, preferred_element_type=F32
                 )
+
+            @pl.when(jnp.logical_and(step == 0, turn == 0))
+            def _():
+                pl.semaphore_wait(barrier, devices - 1)
+                for ahead in range(1, groups):
+                    for copy in gather(ahead):
+                        copy.start()
+
             return 0
 
         lax.fori_loop(0, dates // unroll, some_dates, 0)
@@ -268,7 +313,7 @@
             every = every + inbox_ref[q, s]
     mean = jnp.sum(jnp.where(small == 2 * count, every, 0.0), axis=1, keepdims=True)
     mean = mean / (shocks * across)
-    part = jnp.concatenate([pd_ref[...]] * shocks + own + [rest], axis=1) * mine
+    part = jnp.concatenate([pd_all[me_p]] * shocks + own + [rest], axis=1) * mine
     for s in range(shocks):
         adjustment = jnp.sum(jnp.where(of_shock(s), part, 0.0), axis=1, keepdims=True)
         mine = jnp.where(small == 2 * count + 1 + shocks + s, adjustment - mean, mine)
@@ -296,13 +341,20 @@
     across = lax.axis_size("sa")
     local = trade_weights.shape[1]
     vmem = pl.BlockSpec(memory_space=pltpu.VMEM)
-    smem = pl.BlockSpec(memory_space=pltpu.SMEM)
+    hbm = pl.BlockSpec(memory_space=pltpu.HBM)
     result = pl.pallas_call(
         functools.partial(kernel, groups, across),
         out_shape=jax.ShapeDtypeStruct((owned, 128), F32),
-        in_specs=[smem] + [vmem] * 9,
+        in_specs=[hbm] * 10,
         out_specs=vmem,
         scratch_shapes=[
+            pltpu.SMEM(shock_pick.shape, jnp.int32),
+            pltpu.VMEM(factors.shape, BF),
+            pltpu.VMEM((1, sets), jnp.int32),
+            pltpu.VMEM(shock_scale.shape, F32),
+            pltpu.VMEM(shock_shift.shape, F32),
+            pltpu.VMEM(discount.shape, BF),
+            pltpu.VMEM((1, dates), F32),
             pltpu.VMEM((count * dates, paths), F32),
             pltpu.VMEM((KDIM, dates * shocks * paths), BF),
             pltpu.VMEM((local, KDIM), BF),
@@ -317,9 +369,10 @@
             pltpu.SemaphoreType.DMA((3, groups)),
             pltpu.SemaphoreType.DMA((groups * across,)),
             pltpu.SemaphoreType.DMA((groups * across,)),
+            pltpu.SemaphoreType.DMA((7,)),
         ],
         compiler_params=pltpu.CompilerParams(
-            vmem_limit_bytes=48 * 1024 * 1024, collective_id=0, has_side_effects=True
+            collective_id=0, has_side_effects=True
         ),
     )(
         shock_pick,

time: 71.8 us -> 60.2 us (0.84)
  Pallas kernels: 63.4 us -> 56.7 us
  local copies, waits for them, and re-layouts: 7.32 us -> 2.73 us
    pallas_call x1, Pallas kernels: 63.4 us -> 56.7 us  [on_device(): pl.pallas_call(functools.partial(kernel, groups, across), out_shape=jax.S...]
    unnamed x21 -> x3, local copies, waits for them, and re-layouts: 5.98 us -> 0.66 us
    squeeze x1, local copies, waits for them, and re-layouts: 0.58 us -> 1.32 us  [on_device(): total_xva = result[0, 2 * lanes + 1:2 * lanes + 1 + shocks]]
where the time goes in v2:
time: 60.2 us; the launch traced here: 60.1 us
  Pallas kernels  56.7 us (94%)
  local copies, waits for them, and re-layouts  2.73 us (5%)
  between operations  0.65 us (1%)
    pallas_call x1, Pallas kernels, on_device(): pl.pallas_call(functools.partial(kernel, groups, across), out_shape=jax.S...  56.7 us
    squeeze x1, local copies, waits for them, and re-layouts, on_device(): total_xva = result[0, 2 * lanes + 1:2 * lanes + 1 + shocks]  1.32 us

profile of v2, /device:TPU:0, one launch (start us, length us, event | category | flops | bytes accessed | tf_op | source)
XLA Modules:
  0.0 60.1 jit_solution(6650307934666184471)
XLA Ops:
  0.6 56.7 %shard_map.121 = f32[4,128]{1,0:T(4,128)} custom-call(s32[2]{0:T(128)} %pick_hbm.1, bf16[64,16,128]{2,1,0:T(8,128)(2,1)} %factor_hbm.1, bf16[64,1024]{1,0:T(8,128)(2,1)} %weight_hbm.1, bf16[2,1024]{1,0:T(2,128)(2,1)} %term_hbm.1, s32[1,32]{1,0:T(1,128)} %bitcast.10, f32[32,64]{1,0:T(8,128)} %scale_hbm.1, f32[32,64]{1,0:T(8,128)} %shift_hbm.1, ...), custom_call_target="tpu_custom_call" | custom-call | tf_op jit(solution)/shard_map/pallas_call | solution.py:345
  57.3 0.0 copy-start
  57.3 1.3 %slice_bitcast_fusion = f32[2]{0:T(128)} fusion(f32[4,128]{1,0:T(4,128)} %shard_map.121), kind=kLoop, calls=%fused_computation.1 | loop fusion | bytes 16 | tf_op jit(solution)/shard_map/squeeze | solution.py:392
  58.7 0.0 copy-done
  58.7 0.1 slice.10
  58.7 0.7 %copy.14 = f32[4,2]{0,1:T(2,128)} copy(f32[4,2]{1,0:T(4,128)S(1)} %slice.10) | data formatting | bytes 64
  59.4 0.1 reshape.9
  59.5 0.6 %copy.16 = f32[4,2,2,16]{3,2,0,1:T(2,128)} copy(f32[4,2,2,16]{3,2,1,0:T(2,128)S(1)} %reshape.9) | data formatting | bytes 2048 | tf_op jit(solution)/shard_map/reshape | solution.py:390
Async XLA Ops:
  57.3 1.3 %copy-start = (f32[4,128]{1,0:T(4,128)S(1)}, f32[4,128]{1,0:T(4,128)}, u32[]{:S(2)}) copy-start(f32[4,128]{1,0:T(4,128)} %shard_map.121) | copy-start | bytes 6148

commit v3 on v2

--- a/solution.py
+++ b/solution.py
@@ -53,11 +53,9 @@
     high = strike.astype(BF).astype(F32)
     low = strike - high
     width = weights.shape[1]
-    rest = jnp.zeros((KDIM - factors - 8, width), F32)
-    row = lax.broadcasted_iota(jnp.int32, (8, width), 0)
-    tail = jnp.where(row == 0, high, jnp.where(row == 1, low, 0.0))
-    stack = jnp.concatenate([weights.astype(F32), tail, rest], axis=0)
-    return stack.T.astype(BF)
+    row = lax.broadcasted_iota(jnp.int32, (KDIM - factors, width), 0)
+    tail = jnp.where(row == 0, high, jnp.where(row == 1, low, 0.0)).astype(BF)
+    return jnp.concatenate([weights, tail], axis=0).T
 
 
 def partner(me, step, groups):
@@ -94,7 +92,9 @@
     discount_hbm,
     pd_hbm,
     own_hbm,
-    out_ref,
+    profile_ref,
+    xva_ref,
+    total_ref,
     pick_ref,
     factor_ref,
     block_ref,
@@ -150,17 +150,15 @@
 
     barrier = pltpu.get_barrier_semaphore()
 
-    def greet(step, _):
-        other = lax.rem(me + step, devices)
+    def greet(place):
         pl.semaphore_signal(
-            barrier,
-            inc=1,
-            device_id=(other // across, lax.rem(other, across)),
-            device_id_type=pl.DeviceIdType.MESH,
+            barrier, inc=1, device_id=place, device_id_type=pl.DeviceIdType.MESH
         )
-        return 0
-
-    lax.fori_loop(1, devices, greet, 0)
+
+    for step in range(1, groups):
+        greet((lax.rem(me_p + step, groups), me_s))
+    for step in range(1, across):
+        greet((me_p, lax.rem(me_s + step, across)))
     for copy in early:
         copy.wait()
     shock_rows(factor_ref, pick_ref, scale_ref, shift_ref, wide_ref, shocked_ref)
@@ -178,6 +176,13 @@
             for n, (source, target) in enumerate(parts)
         ]
 
+    for n, (source, target) in enumerate(parts):
+        pltpu.make_async_copy(source, target.at[me_p], recv_sem.at[n, me_p]).wait()
+    pl.semaphore_wait(barrier, groups + across - 2)
+    for step in range(1, groups):
+        for copy in gather(step):
+            copy.start()
+
     m = lax.broadcasted_iota(jnp.int32, (sets, sets), 0)
     j = lax.broadcasted_iota(jnp.int32, (sets, sets), 1)
     counts = jnp.broadcast_to(block_ref[...].astype(F32), (sets, sets))
@@ -185,13 +190,17 @@
     begins = jnp.sum(jnp.where(j < m, counts, 0.0), axis=1, keepdims=True) * BLOCK
     net_ref[...] = jnp.zeros_like(net_ref)
     wide = shocks * paths
-    unroll = 8 if dates % 8 == 0 else 1
+    unroll = next(n for n in (16, 8, 4, 2, 1) if dates % n == 0)
     sub = min(SUB, local)
 
     def one_slot(step, _):
         slot = partner(me_p, step, groups)
-        for n, (source, target) in enumerate(parts):
-            pltpu.make_async_copy(source, target.at[slot], recv_sem.at[n, slot]).wait()
+
+        @pl.when(step > 0)
+        def _():
+            for n, (source, target) in enumerate(parts):
+                pltpu.make_async_copy(source, target.at[slot], recv_sem.at[n, slot]).wait()
+
         terms = term_all[slot]
         loading_ref[...] = load_trades(weight_all[slot], terms, factors)
         ids = lax.broadcasted_iota(jnp.int32, (sets, local), 1) + slot * local
@@ -214,14 +223,6 @@
                 net_ref[:, pl.ds(at, wide)] += jnp.dot(
                     member_ref[...], whole, preferred_element_type=F32
                 )
-
-            @pl.when(jnp.logical_and(step == 0, turn == 0))
-            def _():
-                pl.semaphore_wait(barrier, devices - 1)
-                for ahead in range(1, groups):
-                    for copy in gather(ahead):
-                        copy.start()
-
             return 0
 
         lax.fori_loop(0, dates // unroll, some_dates, 0)
@@ -314,10 +315,17 @@
     mean = jnp.sum(jnp.where(small == 2 * count, every, 0.0), axis=1, keepdims=True)
     mean = mean / (shocks * across)
     part = jnp.concatenate([pd_all[me_p]] * shocks + own + [rest], axis=1) * mine
+    for half in range(2):
+        for s in range(shocks):
+            at = half * count + s * dates
+            profile_ref[half, :, s, :] = mine[:, at : at + dates]
+    diagonal = small == lax.broadcasted_iota(jnp.int32, (owned, 128), 0)
     for s in range(shocks):
         adjustment = jnp.sum(jnp.where(of_shock(s), part, 0.0), axis=1, keepdims=True)
-        mine = jnp.where(small == 2 * count + 1 + shocks + s, adjustment - mean, mine)
-    out_ref[...] = mine
+        line = jnp.sum(jnp.where(diagonal, adjustment - mean, 0.0), axis=0, keepdims=True)
+        xva_ref[s : s + 1, :] = line[:, :owned]
+    at = 2 * count + 1
+    total_ref[...] = mine[0:1, at : at + shocks]
     lax.fori_loop(1, devices, done_one, 0)
 
 
@@ -342,11 +350,15 @@
     local = trade_weights.shape[1]
     vmem = pl.BlockSpec(memory_space=pltpu.VMEM)
     hbm = pl.BlockSpec(memory_space=pltpu.HBM)
-    result = pl.pallas_call(
+    profile, set_xva, total_xva = pl.pallas_call(
         functools.partial(kernel, groups, across),
-        out_shape=jax.ShapeDtypeStruct((owned, 128), F32),
+        out_shape=(
+            jax.ShapeDtypeStruct((2, owned, shocks, dates), F32),
+            jax.ShapeDtypeStruct((shocks, owned), F32),
+            jax.ShapeDtypeStruct((1, shocks), F32),
+        ),
         in_specs=[hbm] * 10,
-        out_specs=vmem,
+        out_specs=(vmem, vmem, vmem),
         scratch_shapes=[
             pltpu.SMEM(shock_pick.shape, jnp.int32),
             pltpu.VMEM(factors.shape, BF),
@@ -386,12 +398,7 @@
         set_pd,
         own_pd[None, :],
     )
-    lanes = dates * shocks
-    profile = result[:, : 2 * lanes].reshape(owned, 2, shocks, dates)
-    profile = profile.transpose(1, 0, 3, 2)
-    total_xva = result[0, 2 * lanes + 1 : 2 * lanes + 1 + shocks]
-    set_xva = result[:, 2 * lanes + 1 + shocks : 2 * lanes + 1 + 2 * shocks]
-    return (profile, set_xva, total_xva)
+    return (profile.transpose(0, 1, 3, 2), set_xva.T, total_xva[0])
 
 
 def solution(mesh):

time: 60.2 us -> 55.3 us (0.919)
  Pallas kernels: 56.7 us -> 51.9 us
    pallas_call x1, Pallas kernels: 56.7 us -> 51.9 us  [on_device(): pl.pallas_call(functools.partial(kernel, groups, across), out_shape=(jax....]
    unnamed x3 -> x9, local copies, waits for them, and re-layouts: 0.66 us -> 2.43 us
    squeeze x1 -> x0, local copies, waits for them, and re-layouts: 1.32 us -> none  [on_device(): total_xva = result[0, 2 * lanes + 1:2 * lanes + 1 + shocks]]
    reshape x2 -> x0, local copies, waits for them, and re-layouts: 0.69 us -> none  [on_device(): profile = result[:, :2 * lanes].reshape(owned, 2, shocks, dates)]
where the time goes in v3:
time: 55.3 us; the launch traced here: 55 us
  Pallas kernels  51.9 us (94%)
  local copies, waits for them, and re-layouts  2.43 us (4%)
  between operations  0.65 us (1%)
    pallas_call x1, Pallas kernels, on_device(): pl.pallas_call(functools.partial(kernel, groups, across), out_shape=(jax....  51.9 us
    unnamed x9, local copies, waits for them, and re-layouts  2.43 us

profile of v3, /device:TPU:0, one launch (start us, length us, event | category | flops | bytes accessed | tf_op | source)
XLA Modules:
  0.0 55.0 jit_solution(6460808968313432991)
XLA Ops:
  0.6 51.9 %shard_map.121 = (f32[2,4,2,16]{3,2,1,0:T(2,128)}, f32[2,4]{1,0:T(2,128)}, f32[1,2]{1,0:T(1,128)}) custom-call(s32[2]{0:T(128)} %pick_hbm.1, bf16[64,16,128]{2,1,0:T(8,128)(2,1)} %factor_hbm.1, bf16[64,1024]{1,0:T(8,128)(2,1)} %weight_hbm.1, bf16[2,1024]{1,0:T(2,128)(2,1)} %term_hbm.1, s32[1,32]{1,0:T(1,128)} %bitcast.7, f32[32,64]{1,0:T(8,128)} %scale_hbm.1, ...), custom_call_target="tpu_custom_call" | custom-call | tf_op jit(solution)/shard_map/pallas_call | solution.py:353
  52.6 0.0 copy-start
  52.6 0.7 %copy-done = f32[2,4,2,16]{3,2,1,0:T(2,128)S(1)} copy-done((f32[2,4,2,16]{3,2,1,0:T(2,128)S(1)}, f32[2,4,2,16]{3,2,1,0:T(2,128)}, u32[]{:S(2)}) %copy-start) | copy-done | bytes 1048
  53.3 0.0 copy-start.1
  53.3 0.6 %copy.16 = f32[2,4,16,2]{2,3,1,0:T(2,128)} copy(f32[2,4,16,2]{2,3,1,0:T(2,128)S(1)} %bitcast.5) | data formatting | bytes 2048
  53.9 0.0 copy-done.1
  53.9 0.0 copy-start.2
  53.9 0.6 %copy.17 = f32[4,2]{0,1:T(2,128)} copy(f32[4,2]{0,1:T(2,128)S(1)} %bitcast.6) | data formatting | bytes 64
  54.5 0.0 copy-done.2
  54.5 0.5 copy.18
Async XLA Ops:
  52.6 0.7 %copy-start = (f32[2,4,2,16]{3,2,1,0:T(2,128)S(1)}, f32[2,4,2,16]{3,2,1,0:T(2,128)}, u32[]{:S(2)}) copy-start(f32[2,4,2,16]{3,2,1,0:T(2,128)} %get-tuple-element.6) | copy-start | bytes 3076
  53.3 0.6 %copy-start.1 = (f32[2,4]{1,0:T(2,128)S(1)}, f32[2,4]{1,0:T(2,128)}, u32[]{:S(2)}) copy-start(f32[2,4]{1,0:T(2,128)} %get-tuple-element.7) | copy-start | bytes 100
  53.9 0.6 %copy-start.2 = (f32[1,2]{1,0:T(1,128)S(1)}, f32[1,2]{1,0:T(1,128)}, u32[]{:S(2)}) copy-start(f32[1,2]{1,0:T(1,128)} %get-tuple-element.8) | copy-start | bytes 28

commit v4 on v3

--- a/solution.py
+++ b/solution.py
@@ -92,9 +92,7 @@
     discount_hbm,
     pd_hbm,
     own_hbm,
-    profile_ref,
-    xva_ref,
-    total_ref,
+    out_ref,
     pick_ref,
     factor_ref,
     block_ref,
@@ -159,10 +157,6 @@
         greet((lax.rem(me_p + step, groups), me_s))
     for step in range(1, across):
         greet((me_p, lax.rem(me_s + step, across)))
-    for copy in early:
-        copy.wait()
-    shock_rows(factor_ref, pick_ref, scale_ref, shift_ref, wide_ref, shocked_ref)
-
     def gather(step):
         other = partner(me_p, step if not groups & (groups - 1) else groups - step, groups)
         return [
@@ -182,6 +176,9 @@
     for step in range(1, groups):
         for copy in gather(step):
             copy.start()
+    for copy in early:
+        copy.wait()
+    shock_rows(factor_ref, pick_ref, scale_ref, shift_ref, wide_ref, shocked_ref)
 
     m = lax.broadcasted_iota(jnp.int32, (sets, sets), 0)
     j = lax.broadcasted_iota(jnp.int32, (sets, sets), 1)
@@ -270,63 +267,58 @@
         for s in range(shocks):
             block = jnp.where(small == 2 * count + 1 + s, totals[s], block)
         message_ref[q] = block
-    inbox_ref[me_p, me_s] = message_ref[me_p]
-
-    def post(step):
-        other = lax.rem(me + step, devices)
-        other_p = other // across
-        return send(
-            message_ref.at[other_p],
-            inbox_ref.at[me_p, me_s],
-            post_sem.at[step],
-            inbox_sem.at[me],
-            (other_p, lax.rem(other, across)),
-        )
-
-    def post_one(step, _):
-        post(step).start()
-        return 0
-
-    def take_one(step, _):
-        source = lax.rem(me + step, devices)
-        pltpu.make_async_copy(
-            message_ref.at[0],
-            inbox_ref.at[source // across, lax.rem(source, across)],
-            inbox_sem.at[source],
-        ).wait()
-        return 0
-
-    def done_one(step, _):
-        post(step).wait_send()
-        return 0
-
-    lax.fori_loop(1, devices, post_one, 0)
+    inbox_ref[me] = message_ref[me_p]
+
+    for far_p in reversed(range(groups)):
+        for far_s in reversed(range(across)):
+            if far_p + far_s:
+                other_p = partner(me_p, far_p, groups)
+                send(
+                    message_ref.at[other_p],
+                    inbox_ref.at[me],
+                    post_sem,
+                    inbox_sem,
+                    (other_p, partner(me_s, far_s, across)),
+                ).start()
     for step in range(1, groups):
         for copy in gather(step):
             copy.wait_send()
-    lax.fori_loop(1, devices, take_one, 0)
+    others = inbox_ref.at[pl.ds(0, devices - 1)]
+    pltpu.make_async_copy(others, others, inbox_sem).wait()
 
     mine = jnp.zeros((owned, 128), F32)
     every = jnp.zeros((owned, 128), F32)
     for q in range(groups):
-        mine = mine + inbox_ref[q, me_s]
+        mine = mine + inbox_ref[q * across + me_s]
         for s in range(across):
-            every = every + inbox_ref[q, s]
+            every = every + inbox_ref[q * across + s]
     mean = jnp.sum(jnp.where(small == 2 * count, every, 0.0), axis=1, keepdims=True)
     mean = mean / (shocks * across)
     part = jnp.concatenate([pd_all[me_p]] * shocks + own + [rest], axis=1) * mine
+    for s in range(shocks):
+        adjustment = jnp.sum(jnp.where(of_shock(s), part, 0.0), axis=1, keepdims=True)
+        mine = jnp.where(small == 2 * count + 1 + shocks + s, adjustment - mean, mine)
+    out_ref[...] = mine
+    pltpu.make_async_copy(others, others, post_sem).wait()
+
+
+def split(mine_ref, profile_ref, xva_ref, total_ref):
+    owned, shocks, dates = profile_ref.shape[1:]
+    count = dates * shocks
+    mine = mine_ref[...]
     for half in range(2):
         for s in range(shocks):
             at = half * count + s * dates
             profile_ref[half, :, s, :] = mine[:, at : at + dates]
-    diagonal = small == lax.broadcasted_iota(jnp.int32, (owned, 128), 0)
-    for s in range(shocks):
-        adjustment = jnp.sum(jnp.where(of_shock(s), part, 0.0), axis=1, keepdims=True)
-        line = jnp.sum(jnp.where(diagonal, adjustment - mean, 0.0), axis=0, keepdims=True)
-        xva_ref[s : s + 1, :] = line[:, :owned]
+    row = lax.broadcasted_iota(jnp.int32, (owned, owned), 0)
+    diagonal = row == lax.broadcasted_iota(jnp.int32, (owned, owned), 1)
     at = 2 * count + 1
     total_ref[...] = mine[0:1, at : at + shocks]
-    lax.fori_loop(1, devices, done_one, 0)
+    for s in range(shocks):
+        column = mine[:, at + shocks + s : at + shocks + s + 1]
+        xva_ref[s : s + 1, :] = jnp.sum(
+            jnp.where(diagonal, column, 0.0), axis=0, keepdims=True
+        )
 
 
 def on_device(
@@ -350,15 +342,11 @@
     local = trade_weights.shape[1]
     vmem = pl.BlockSpec(memory_space=pltpu.VMEM)
     hbm = pl.BlockSpec(memory_space=pltpu.HBM)
-    profile, set_xva, total_xva = pl.pallas_call(
+    result = pl.pallas_call(
         functools.partial(kernel, groups, across),
-        out_shape=(
-            jax.ShapeDtypeStruct((2, owned, shocks, dates), F32),
-            jax.ShapeDtypeStruct((shocks, owned), F32),
-            jax.ShapeDtypeStruct((1, shocks), F32),
-        ),
+        out_shape=jax.ShapeDtypeStruct((owned, 128), F32),
         in_specs=[hbm] * 10,
-        out_specs=(vmem, vmem, vmem),
+        out_specs=vmem,
         scratch_shapes=[
             pltpu.SMEM(shock_pick.shape, jnp.int32),
             pltpu.VMEM(factors.shape, BF),
@@ -376,11 +364,11 @@
             pltpu.VMEM((groups,) + payoff_terms.shape, BF),
             pltpu.VMEM((groups,) + set_pd.shape, F32),
             pltpu.VMEM((groups, owned, 128), F32),
-            pltpu.VMEM((groups, across, owned, 128), F32),
+            pltpu.VMEM((groups * across, owned, 128), F32),
             pltpu.SemaphoreType.DMA((3, groups)),
             pltpu.SemaphoreType.DMA((3, groups)),
-            pltpu.SemaphoreType.DMA((groups * across,)),
-            pltpu.SemaphoreType.DMA((groups * across,)),
+            pltpu.SemaphoreType.DMA,
+            pltpu.SemaphoreType.DMA,
             pltpu.SemaphoreType.DMA((7,)),
         ],
         compiler_params=pltpu.CompilerParams(
@@ -398,6 +386,16 @@
         set_pd,
         own_pd[None, :],
     )
+    profile, set_xva, total_xva = pl.pallas_call(
+        split,
+        out_shape=(
+            jax.ShapeDtypeStruct((2, owned, shocks, dates), F32),
+            jax.ShapeDtypeStruct((shocks, owned), F32),
+            jax.ShapeDtypeStruct((1, shocks), F32),
+        ),
+        in_specs=[vmem],
+        out_specs=(vmem, vmem, vmem),
+    )(result)
     return (profile.transpose(0, 1, 3, 2), set_xva.T, total_xva[0])
 
 

time: 55.3 us -> 53.2 us (0.962)
  local copies, waits for them, and re-layouts: 2.43 us -> 0 us
    unnamed x9 -> x0, local copies, waits for them, and re-layouts: 2.43 us -> none
    pallas_call x1 -> x2, Pallas kernels: 51.9 us -> 52.4 us  [the longest x1 51 us: on_device(): pl.pallas_call(functools.partial(kernel, groups, across), out_shape=jax.S...]
where the time goes in v4:
time: 53.2 us; the launch traced here: 53 us
  Pallas kernels  52.4 us (98%)
  between operations  0.64 us (1%)
    pallas_call x1, Pallas kernels, on_device(): pl.pallas_call(functools.partial(kernel, groups, across), out_shape=jax.S...  51 us
    pallas_call x1, Pallas kernels, on_device(): pl.pallas_call(split, out_shape=(jax.ShapeDtypeStruct((2, owned, shocks,...  1.36 us

profile of v4, /device:TPU:0, one launch (start us, length us, event | category | flops | bytes accessed | tf_op | source)
XLA Modules:
  0.0 53.0 jit_solution(17735917785257158322)
XLA Ops:
  0.6 51.0 %shard_map.121.mine_ref = f32[4,128]{1,0:T(4,128)} custom-call(s32[2]{0:T(128)} %pick_hbm.1, bf16[64,16,128]{2,1,0:T(8,128)(2,1)} %factor_hbm.1, bf16[64,1024]{1,0:T(8,128)(2,1)} %weight_hbm.1, bf16[2,1024]{1,0:T(2,128)(2,1)} %term_hbm.1, s32[1,32]{1,0:T(1,128)} %bitcast.5, f32[32,64]{1,0:T(8,128)} %scale_hbm.1, f32[32,64]{1,0:T(8,128)} %shift_hbm.1, ...), custom_call_target="tpu_custom_call" | custom-call | tf_op jit(solution)/shard_map/pallas_call | solution.py:345
  51.6 1.4 %shard_map.122 = (f32[2,4,2,16]{3,2,1,0:T(2,128)}, f32[2,4]{1,0:T(2,128)}, f32[1,2]{1,0:T(1,128)}) custom-call(f32[4,128]{1,0:T(4,128)} %shard_map.121.mine_ref), custom_call_target="tpu_custom_call" | custom-call | tf_op jit(solution)/shard_map/pallas_call | solution.py:389

commit v5 on v4

--- a/solution.py
+++ b/solution.py
@@ -126,6 +126,18 @@
     me_p = lax.axis_index("pa")
     me_s = lax.axis_index("sa")
     me = me_p * across + me_s
+    barrier = pltpu.get_barrier_semaphore()
+
+    def greet(place):
+        pl.semaphore_signal(
+            barrier, inc=1, device_id=place, device_id_type=pl.DeviceIdType.MESH
+        )
+
+    for step in range(1, groups):
+        greet((lax.rem(me_p + step, groups), me_s))
+    for step in range(1, across):
+        greet((me_p, lax.rem(me_s + step, across)))
+
     parts = ((weight_hbm, weight_all), (term_hbm, term_all), (pd_hbm, pd_all))
     early = [
         pltpu.make_async_copy(source, target, load_sem.at[n])
@@ -146,24 +158,13 @@
     for n, (source, target) in enumerate(parts):
         pltpu.make_async_copy(source, target.at[me_p], recv_sem.at[n, me_p]).start()
 
-    barrier = pltpu.get_barrier_semaphore()
-
-    def greet(place):
-        pl.semaphore_signal(
-            barrier, inc=1, device_id=place, device_id_type=pl.DeviceIdType.MESH
-        )
-
-    for step in range(1, groups):
-        greet((lax.rem(me_p + step, groups), me_s))
-    for step in range(1, across):
-        greet((me_p, lax.rem(me_s + step, across)))
     def gather(step):
         other = partner(me_p, step if not groups & (groups - 1) else groups - step, groups)
         return [
             send(
                 target.at[me_p],
                 target.at[me_p],
-                send_sem.at[n, step],
+                send_sem.at[n],
                 recv_sem.at[n, me_p],
                 (other, me_s),
             )
@@ -280,9 +281,9 @@
                     inbox_sem,
                     (other_p, partner(me_s, far_s, across)),
                 ).start()
-    for step in range(1, groups):
-        for copy in gather(step):
-            copy.wait_send()
+    for n, (source, target) in enumerate(parts):
+        gone = target.at[pl.ds(0, groups - 1)]
+        pltpu.make_async_copy(gone, gone, send_sem.at[n]).wait()
     others = inbox_ref.at[pl.ds(0, devices - 1)]
     pltpu.make_async_copy(others, others, inbox_sem).wait()
 
@@ -365,7 +366,7 @@
             pltpu.VMEM((groups,) + set_pd.shape, F32),
             pltpu.VMEM((groups, owned, 128), F32),
             pltpu.VMEM((groups * across, owned, 128), F32),
-            pltpu.SemaphoreType.DMA((3, groups)),
+            pltpu.SemaphoreType.DMA((3,)),
             pltpu.SemaphoreType.DMA((3, groups)),
             pltpu.SemaphoreType.DMA,
             pltpu.SemaphoreType.DMA,

time: 53.2 us -> 53 us (level)
  no operation moved by 1% of the time
where the time goes in v5:
time: 53 us; the launch traced here: 52.8 us
  Pallas kernels  52.2 us (98%)
  between operations  0.64 us (1%)
    pallas_call x1, Pallas kernels, on_device(): pl.pallas_call(functools.partial(kernel, groups, across), out_shape=jax.S...  50.8 us
    pallas_call x1, Pallas kernels, on_device(): pl.pallas_call(split, out_shape=(jax.ShapeDtypeStruct((2, owned, shocks,...  1.36 us

profile of v5, /device:TPU:0, one launch (start us, length us, event | category | flops | bytes accessed | tf_op | source)
XLA Modules:
  0.0 52.8 jit_solution(16117390244996285829)
XLA Ops:
  0.6 50.8 %shard_map.121.mine_ref = f32[4,128]{1,0:T(4,128)} custom-call(s32[2]{0:T(128)} %pick_hbm.1, bf16[64,16,128]{2,1,0:T(8,128)(2,1)} %factor_hbm.1, bf16[64,1024]{1,0:T(8,128)(2,1)} %weight_hbm.1, bf16[2,1024]{1,0:T(2,128)(2,1)} %term_hbm.1, s32[1,32]{1,0:T(1,128)} %bitcast.5, f32[32,64]{1,0:T(8,128)} %scale_hbm.1, f32[32,64]{1,0:T(8,128)} %shift_hbm.1, ...), custom_call_target="tpu_custom_call" | custom-call | tf_op jit(solution)/shard_map/pallas_call | solution.py:346
  51.4 1.4 %shard_map.122 = (f32[2,4,2,16]{3,2,1,0:T(2,128)}, f32[2,4]{1,0:T(2,128)}, f32[1,2]{1,0:T(1,128)}) custom-call(f32[4,128]{1,0:T(4,128)} %shard_map.121.mine_ref), custom_call_target="tpu_custom_call" | custom-call | tf_op jit(solution)/shard_map/pallas_call | solution.py:390
